TPU v7x, 32 devices: a whole 2x2x4 slice. The times are simulated.
32 devices in a mesh: dp: 4 (over x, y), tp: 8 (over z, core).
Axes of the slice: x: 2, y: 2, z: 4, core: 2. Of those that a mesh axis runs over, the one named last changes fastest.
Arguments:
- x: bfloat16 [16384, 2048], P(('dp', 'tp')), parts along dimension 0
- dy: bfloat16 [16384, 2048], P(('dp', 'tp')), parts along dimension 0
- gate: bfloat16 [16384, 8192], P('dp', 'tp'), parts along dimension 0
- up: bfloat16 [16384, 8192], P('dp', 'tp'), parts along dimension 0
- w_gate: bfloat16 [2048, 8192], P(None, 'tp')
- w_up: bfloat16 [2048, 8192], P(None, 'tp')
- w_down: bfloat16 [8192, 2048], P('tp')
Outputs:
- output 1: bfloat16 [16384, 2048], P(('dp', 'tp')), parts along dimension 0
- output 2: bfloat16 [8192, 8192], P('dp', 'tp'), parts along dimension 0
- output 3: bfloat16 [8192, 8192], P('dp', 'tp'), parts along dimension 0
- output 4: bfloat16 [32768, 2048], P(('dp', 'tp')), parts along dimension 0
There are 4 independent parts. A program takes and returns all parts, laid end to end along the dimension named above; an argument that names none is the same for every part.
All inputs are finite; a program needn't handle non-finite values.
Results may differ from a plain program's by a relative error of at most 0.012.
Values are sent between devices in bfloat16 or wider.
A program may use at most 2 GiB of HBM per device.

v0:
```python
import jax
import jax.numpy as jnp


def act(gate, up):
    return jax.nn.silu(gate) * up


def solution(mesh):
    def step(x, dy, gate, up, w_gate, w_up, w_down):
        hidden, back = jax.vjp(act, gate.astype(jnp.float32), up.astype(jnp.float32))
        d_hidden = jnp.dot(dy, w_down.T, preferred_element_type=jnp.float32)
        d_gate, d_up = (g.astype(jnp.bfloat16) for g in back(d_hidden))
        dx = jnp.dot(d_gate, w_gate.T) + jnp.dot(d_up, w_up.T)
        groups = mesh.shape["dp"]

        def by_group(a, b):
            a, b = (t.reshape(groups, -1, t.shape[-1]) for t in (a, b))
            product = jnp.einsum("gta,gtb->gab", a, b, preferred_element_type=jnp.float32)
            return product.astype(jnp.bfloat16).reshape(-1, b.shape[-1])

        return dx, by_group(x, d_gate), by_group(x, d_up), by_group(hidden.astype(jnp.bfloat16), dy)

    return step
```

profile of v0, /device:TPU:0, one launch (start us, length us, event | category | flops | bytes accessed | tf_op | source)
XLA Modules:
  0.0 491.0 jit_solution(11706353400301603448)
XLA Ops:
  7.2 0.0 all-gather.11.cloned.1.call-start
  7.2 0.7 all-gather.11.cloned.1.call-update
  7.9 0.0 all-gather.13.cloned.1.call-start
  7.9 0.7 all-gather.13.cloned.1.call-update
  8.7 0.0 reduce-scatter.4.cloned.1.call-start
  8.7 154.6 %all-gather.11.cloned.1.call-done = bf16[4096,2048]{1,0:T(8,128)(2,1)} async-done(((bf16[512,2048]{1,0:T(8,128)(2,1)}), bf16[4096,2048]{1,0:T(8,128)(2,1)}) %all-gather.11.cloned.1.call-update) | async-done | bytes 16777232 | tf_op args[1]
  163.3 32.7 %multiply_convert_fusion = (bf16[4096,1024]{1,0:T(8,128)(2,1)}, bf16[4096,1024]{1,0:T(8,128)(2,1)}) fusion(bf16[4096,1024]{1,0:T(8,128)(2,1)} %param.3, bf16[4096,1024]{1,0:T(8,128)(2,1)} %param.2, bf16[4096,2048]{1,0:T(8,128)(2,1)} %all-gather.11.cloned.1.call-done, bf16[1024,2048]{1,0:T(8,128)(2,1)} %param.1), kind=kOutput, calls=%fused_computation.13 | convolution fusion | flops 17246978048 | bytes 54525952 | tf_op jit(solution)/dot_general | solution.py:12
  196.0 23.5 %fusion.13 = bf16[4096,2048]{1,0:T(8,128)(2,1)} fusion(bf16[4096,1024]{1,0:T(8,128)(2,1)} %get-tuple-element.5, bf16[2048,1024]{1,0:T(8,128)(2,1)} %param.4), kind=kOutput, calls=%fused_computation.20 | convolution fusion | flops 17179869184 | bytes 29360128 | tf_op jit(solution)/dot_general | solution.py:14
  219.6 25.2 %convolution_add_fusion = bf16[4096,2048]{1,0:T(8,128)(2,1)} fusion(bf16[4096,2048]{1,0:T(8,128)(2,1)} %fusion.13, bf16[4096,1024]{1,0:T(8,128)(2,1)} %get-tuple-element.4, bf16[2048,1024]{1,0:T(8,128)(2,1)} %param.5), kind=kOutput, calls=%fused_computation.14 | convolution fusion | flops 17188257792 | bytes 46137344 | tf_op jit(solution)/dot_general | solution.py:14
  244.7 0.0 reduce-scatter.4.cloned.1.call-update
  244.8 69.9 %all-gather.13.cloned.1.call-done = bf16[4096,2048]{1,0:T(8,128)(2,1)} async-done(((bf16[512,2048]{1,0:T(8,128)(2,1)}), bf16[4096,2048]{1,0:T(8,128)(2,1)}) %all-gather.13.cloned.1.call-update) | async-done | bytes 16777232 | tf_op jit(solution)/reshape | solution.py:18
  314.7 23.8 %convert_bitcast_fusion.1 = bf16[2048,1024]{0,1:T(8,128)(2,1)} fusion(bf16[4096,1024]{1,0:T(8,128)(2,1)} %get-tuple-element.5, bf16[4096,2048]{1,0:T(8,128)(2,1)} %all-gather.13.cloned.1.call-done), kind=kOutput, calls=%fused_computation.17 | convolution fusion | flops 17181966336 | bytes 29360128 | tf_op jit(solution)/gta,gtb->gab/dot_general | solution.py:19
  338.5 6.4 %copy = bf16[2048,1024]{1,0:T(8,128)(2,1)} copy(bf16[2048,1024]{0,1:T(8,128)(2,1)} %convert_bitcast_fusion.1) | data formatting | bytes 8388608
  344.9 23.8 %convert_bitcast_fusion = bf16[2048,1024]{0,1:T(8,128)(2,1)} fusion(bf16[4096,1024]{1,0:T(8,128)(2,1)} %get-tuple-element.4, bf16[4096,2048]{1,0:T(8,128)(2,1)} %all-gather.13.cloned.1.call-done), kind=kOutput, calls=%fused_computation.16 | convolution fusion | flops 17181966336 | bytes 29360128 | tf_op jit(solution)/gta,gtb->gab/dot_general | solution.py:19
  368.6 6.4 %copy.1 = bf16[2048,1024]{1,0:T(8,128)(2,1)} copy(bf16[2048,1024]{0,1:T(8,128)(2,1)} %convert_bitcast_fusion) | data formatting | bytes 8388608
  375.0 27.1 %fusion.9 = bf16[1024,2048]{1,0:T(8,128)(2,1)} fusion(bf16[4096,2048]{1,0:T(8,128)(2,1)} %all-gather.11.cloned.1.call-done, bf16[4096,1024]{1,0:T(8,128)(2,1)} %param.2, bf16[4096,1024]{1,0:T(8,128)(2,1)} %param.3), kind=kOutput, calls=%fused_computation.18 | convolution fusion | flops 17215520768 | bytes 37748736 | tf_op jit(solution)/gta,gtb->gab/dot_general | solution.py:19
  402.1 82.3 %reduce-scatter.4.cloned.1.call-done = bf16[512,2048]{1,0:T(8,128)(2,1)} async-done(((bf16[4096,2048]{1,0:T(8,128)(2,1)}), bf16[512,2048]{1,0:T(8,128)(2,1)}) %reduce-scatter.4.cloned.1.call-update) | async-done | bytes 2097168
Async XLA Ops:
  7.2 156.2 %all-gather.11.cloned.1.call-start = ((), (), s32[]{:S(2)}) async-start(), calls=%async_computation.1 | async-start | bytes 18874368 | tf_op args[1]
  7.9 306.8 %all-gather.13.cloned.1.call-start = ((), (), s32[]{:S(2)}) async-start(), calls=%async_computation.2 | async-start | bytes 18874368 | tf_op jit(solution)/reshape | solution.py:18
  8.7 475.8 %reduce-scatter.4.cloned.1.call-start = ((), (), s32[]{:S(2)}) async-start(), calls=%async_computation.3 | async-start | bytes 18874368
Sparse Core Ops, SparseCore 0:
  9.6 153.7 all-gather.10
  164.9 149.7 all-gather.12
  317.6 166.7 reduce-scatter.3
where the time goes:
time: 491 us
  waiting for transfers between devices  308 us (63%)
  matrix products  156 us (32%)
  between operations  13.7 us (3%)
  local copies, waits for them, and re-layouts  12.8 us (3%)
    unnamed x5, waiting for transfers between devices  238 us
    dot_general x3, matrix products, by_group(): jnp.einsum('gta,gtb->gab', a, b, preferred_element_type=jnp.float32)  74.6 us
    reshape x1, waiting for transfers between devices, by_group(): a, b = (t.reshape(groups, -1, t.shape[-1]) for t in (a, b))  69.9 us
    dot_general x2, matrix products, step(): dx = jnp.dot(d_gate, w_gate.T) + jnp.dot(d_up, w_up.T)  48.7 us
    dot_general x1, matrix products, step(): d_hidden = jnp.dot(dy, w_down.T, preferred_element_type=jnp.float32)  32.7 us
    unnamed x2, local copies, waits for them, and re-layouts  12.8 us
  transfers between devices with their start and end apart: 3, of which 3 were waited for; matrix products, arithmetic and copies ran while one was open for 34% of the time, Pallas kernels for 0%

commit v1 on v0

v1 whole, which is shorter than its diff:
```python
import functools

import jax
import jax.numpy as jnp
from jax import lax
from jax.experimental import pallas as pl
from jax.experimental.pallas import tpu as pltpu
from jax.sharding import PartitionSpec as P

MESH = pl.DeviceIdType.MESH
CHUNKS = 2
TILE = 256
CHIPS = 4
NT = (((1,), (1,)), ((), ()))
TN = (((0,), (0,)), ((), ()))
X, FORWARD, REDUCE, WRITE_GU, WRITE_DOWN = range(5)
END_STEPS = (
    (REDUCE, 0), (REDUCE, 1), (WRITE_DOWN, 0), (X, 0), (X, 1), (FORWARD, 1), (X, 2), (X, 3), (REDUCE, 2),
    (FORWARD, 2), (X, 4), (X, 5), (FORWARD, 3), (X, 6), (X, 7), (WRITE_GU, 0), (REDUCE, 3),
)
MIDDLE_STEPS = (
    (WRITE_DOWN, 0), (X, 0), (X, 1), (FORWARD, 1), (X, 2), (X, 3), (X, 4), (X, 5), (FORWARD, 2),
    (X, 6), (X, 7), (FORWARD, 3), (REDUCE, 0), (REDUCE, 1), (REDUCE, 2), (WRITE_GU, 0), (REDUCE, 3),
)


def pick(table, i):
    value = jnp.int32(table[0])
    for j in range(1, len(table)):
        value = jnp.where(i == j, jnp.int32(table[j]), value)
    return value


def dot(a, b, dims):
    return lax.dot_general(a, b, dims, preferred_element_type=jnp.float32)


def kernel(
    x, dy, gate, up, w_gate, w_up, w_down,
    dx, dw_gate, dw_up, dw_down, dy_all, x_all, from_partner, from_below, from_above,
    wg, wu, wd, dg, du, acc1, acc2, tok, gv, uv, hid, st,
    w_sem, tok_sem, gate_sem, out_sem, recv_sem, send_sem, partner_sem, below_sem, above_sem, st_sem,
):
    rows, depth = x.shape
    width = gate.shape[1]
    part = rows // CHUNKS
    me = lax.axis_index("tp")
    z, c = me // 2, lax.rem(me, 2)
    other = 1 - c
    last = CHIPS - 1
    is_end = (z == 0) | (z == last)
    low = z < CHIPS // 2
    has_below, has_above = z > 0, z < last
    partner, below, above = {"tp": 2 * z + other}, {"tp": 2 * (z - 1) + c}, {"tp": 2 * (z + 1) + c}

    def mirrored(v):
        return jnp.where(low, v, last - v)

    def arrival(k):
        return mirrored(jnp.where(is_end, k, pick((1, 2, 0, 3), k)))

    def target(r):
        return mirrored(jnp.where(is_end, last - r, pick((3, 0, 2, 1), r)))

    def block_rows(b):
        return pl.ds(pl.multiple_of(b * rows, rows), rows)

    def chunk_rows(b, h):
        return pl.ds(pl.multiple_of(b * rows + h * part, part), part)

    def tile(i, size=TILE):
        return pl.ds(pl.multiple_of(i * size, size), size)

    own = (dy, x)
    whole = (dy_all, x_all)

    def send(t, way, chip, h, device, mine):
        b = 2 * chip + c
        src = own[t].at[pl.ds(h * part, part)] if mine else whole[t].at[chunk_rows(b, h)]
        return pltpu.make_async_remote_copy(
            src_ref=src,
            dst_ref=whole[t].at[chunk_rows(b, h)],
            send_sem=send_sem.at[t, way, chip, h],
            recv_sem=recv_sem.at[t, b, h],
            device_id=device,
            device_id_type=MESH,
        )

    def await_chunk(t, b, h):
        pltpu.make_async_remote_copy(
            src_ref=whole[t].at[chunk_rows(b, h)],
            dst_ref=whole[t].at[chunk_rows(b, h)],
            send_sem=send_sem.at[t, 0, 0, h],
            recv_sem=recv_sem.at[t, b, h],
            device_id=partner,
            device_id_type=MESH,
        ).wait_recv()

    def send_own(t, ways):
        for h in range(CHUNKS):
            for way, device in enumerate((above, below, partner)):
                if ways[way] is True:
                    send(t, way, z, h, device, True).start()
                elif ways[way] is not False:
                    pl.when(ways[way])(lambda t=t, way=way, h=h, device=device: send(t, way, z, h, device, True).start())

    def forward(t, k):
        for h in range(CHUNKS):
            @pl.when(z - k >= 0)
            def _():
                chip = z - k
                await_chunk(t, 2 * chip + c, h)
                pl.when(has_above)(lambda: send(t, 0, chip, h, above, False).start())
                send(t, 2, chip, h, partner, False).start()

            @pl.when(z + k <= last)
            def _():
                chip = z + k
                await_chunk(t, 2 * chip + c, h)
                pl.when(has_below)(lambda: send(t, 1, chip, h, below, False).start())
                send(t, 2, chip, h, partner, False).start()

    def send_x_after(k):
        send_own(1, (has_above & (z == k), has_below & (last - z == k), False))

    barrier = pltpu.get_barrier_semaphore()
    pl.semaphore_signal(barrier, inc=1, device_id=partner, device_id_type=MESH)
    pl.when(has_below)(lambda: pl.semaphore_signal(barrier, inc=1, device_id=below, device_id_type=MESH))
    pl.when(has_above)(lambda: pl.semaphore_signal(barrier, inc=1, device_id=above, device_id_type=MESH))
    pl.semaphore_wait(barrier, jnp.where(is_end, 2, 3))
    send_own(0, (has_above, has_below, True))
    send_x_after(0)
    send_own(1, (False, False, True))

    weights = [pltpu.make_async_copy(a, b, w_sem.at[i]) for i, (a, b) in enumerate(((w_down, wd), (w_gate, wg), (w_up, wu)))]
    for copy in weights:
        copy.start()

    def gate_up(s):
        b = 2 * arrival(s // 2) + jnp.where(lax.rem(s, 2) == 0, c, other)
        slot = lax.rem(s, 2)
        return (
            pltpu.make_async_copy(gate.at[block_rows(b)], gv.at[slot], gate_sem.at[0, slot]),
            pltpu.make_async_copy(up.at[block_rows(b)], uv.at[slot], gate_sem.at[1, slot]),
        )

    for copy in gate_up(jnp.int32(0)):
        copy.start()

    @pl.loop(0, acc1.shape[0] // TILE)
    def _(i):
        acc1[tile(i), :] = jnp.zeros((TILE, width), jnp.float32)

    for copy in weights:
        copy.wait()

    def take_tokens(t, s, b, slot):
        @pl.when(lax.rem(s, 2) == 1)
        def _():
            for h in range(CHUNKS):
                await_chunk(t, b, h)

        @pl.when(s == 0)
        def _():
            pltpu.make_async_copy(own[t], tok.at[slot], tok_sem).start()

        @pl.when(s > 0)
        def _():
            pltpu.make_async_copy(whole[t].at[block_rows(b)], tok.at[slot], tok_sem).start()

        pltpu.make_async_copy(own[t], tok.at[slot], tok_sem).wait()

    def partner_send(chip, h, slot):
        return pltpu.make_async_remote_copy(
            src_ref=st.at[slot],
            dst_ref=from_partner.at[chip, pl.ds(h * part, part)],
            send_sem=st_sem.at[slot],
            recv_sem=partner_sem.at[chip, h],
            device_id=partner,
            device_id_type=MESH,
        )

    @pl.loop(0, 2 * CHIPS)
    def _(s):
        k, odd = s // 2, lax.rem(s, 2)
        chip = arrival(k)
        b = 2 * chip + jnp.where(odd == 0, c, other)
        slot = odd

        for j in range(1, CHIPS):
            @pl.when(s == 2 * j)
            def _(j=j):
                forward(0, j)
                send_x_after(j)

        take_tokens(0, s, b, slot)

        @pl.when(s + 1 < 2 * CHIPS)
        def _():
            for copy in gate_up(s + 1):
                copy.start()

        for copy in gate_up(s):
            copy.wait()

        @pl.loop(0, width // TILE)
        def _(i):
            cols = tile(i)
            d_hidden = dot(tok[slot], wd[cols, :], NT)
            g = gv[slot, :, cols].astype(jnp.float32)
            u = uv[slot, :, cols].astype(jnp.float32)
            s_ = jax.nn.sigmoid(g)
            silu = g * s_
            hid[:, cols] = (silu * u).astype(jnp.bfloat16)
            du[block_rows(b), cols] = (d_hidden * silu).astype(jnp.bfloat16)
            dg[block_rows(b), cols] = (d_hidden * u * (s_ * (1.0 + g * (1.0 - s_)))).astype(jnp.bfloat16)

        @pl.loop(0, width // TILE)
        def _(i):
            left = hid[:, tile(i)]
            acc1[tile(i), :] += dot(left, tok[slot, :, :width], TN)
            acc1[pl.ds(pl.multiple_of(width + i * TILE, TILE), TILE), :] += dot(left, tok[slot, :, width:], TN)

        @pl.when(odd == 1)
        def _():
            base = 2 * lax.rem(k, 2)

            @pl.when(k >= 2)
            def _():
                for h in range(CHUNKS):
                    partner_send(chip, h, base + h).wait_send()

            @pl.loop(0, depth // TILE)
            def _(i):
                term = dot(dg[block_rows(b), :], wg[tile(i), :], NT) + dot(du[block_rows(b), :], wu[tile(i), :], NT)
                for h in range(CHUNKS):
                    st[base + h, :, tile(i)] = term[h * part:(h + 1) * part].astype(jnp.bfloat16)

            for h in range(CHUNKS):
                partner_send(chip, h, base + h).start()

    def x_step(s):
        chip = arrival(s // 2)
        b = 2 * chip + jnp.where(lax.rem(s, 2) == 0, c, other)
        slot = lax.rem(s, 2)
        take_tokens(1, s, b, slot)

        @pl.loop(0, depth // TILE)
        def _(i):
            left = tok[slot, :, tile(i)]
            acc1[tile(i), :] += dot(left, dg[block_rows(b), :], TN)
            acc2[tile(i), :] += dot(left, du[block_rows(b), :], TN)

    def incoming(buffer, sem, chip, h, j):
        piece = buffer.at[chip, tile(h, part)]
        pltpu.make_async_remote_copy(
            src_ref=piece, dst_ref=piece, send_sem=st_sem.at[0], recv_sem=sem.at[chip, h], device_id=partner, device_id_type=MESH
        ).wait_recv()
        copy = pltpu.make_async_copy(piece, wd.at[pl.ds(j * part, part)], tok_sem)
        copy.start()
        copy.wait()

    def reduce_step(r):
        chip = target(r)
        b = 2 * chip + c

        @pl.loop(0, CHUNKS)
        def _(h):
            slot = 2 * lax.rem(r, 2) + h
            partner_send(chip, 0, slot).wait_send()
            incoming(from_partner, partner_sem, chip, h, 0)
            use_below, use_above = (chip >= z) & has_below, (chip <= z) & has_above
            for j, (use, buffer, sem) in enumerate(((use_below, from_below, below_sem), (use_above, from_above, above_sem)), 1):
                pl.when(use)(lambda j=j, buffer=buffer, sem=sem: incoming(buffer, sem, chip, h, j))

                @pl.when(jnp.logical_not(use))
                def _(j=j):
                    wd[j * part:(j + 1) * part, :] = jnp.zeros((part, depth), jnp.bfloat16)

            @pl.loop(0, depth // TILE)
            def _(i):
                here = chunk_rows(b, h)
                total = dot(dg[here, :], wg[tile(i), :], NT) + dot(du[here, :], wu[tile(i), :], NT)
                for j in range(3):
                    total += wd[j * part:(j + 1) * part, tile(i)].astype(jnp.float32)
                st[slot, :, tile(i)] = total.astype(jnp.bfloat16)

            def pass_on(buffer, sem, device):
                pltpu.make_async_remote_copy(
                    src_ref=st.at[slot],
                    dst_ref=buffer.at[chip, tile(h, part)],
                    send_sem=st_sem.at[slot],
                    recv_sem=sem.at[chip, h],
                    device_id=device,
                    device_id_type=MESH,
                ).start()

            pl.when(chip > z)(lambda: pass_on(from_below, below_sem, above))
            pl.when(chip < z)(lambda: pass_on(from_above, above_sem, below))
            pl.when(chip == z)(lambda: pltpu.make_async_copy(st.at[slot], dx.at[tile(h, part)], st_sem.at[slot]).start())

    half = depth // 2
    stage = [gv.at[0], gv.at[1], uv.at[0], uv.at[1]]

    def down_copy(q):
        span = width // 2
        return pltpu.make_async_copy(
            stage[q], dw_down.at[pl.ds((q % 2) * span, span), pl.ds((q // 2) * width, width)], out_sem.at[2 + q]
        )

    def write_down():
        for q in range(4):
            span = width // 2
            stage[q][...] = acc1[q * span:(q + 1) * span, :].astype(jnp.bfloat16)
            down_copy(q).start()

        @pl.loop(0, depth // TILE)
        def _(i):
            acc1[tile(i), :] = jnp.zeros((TILE, width), jnp.float32)
            acc2[tile(i), :] = jnp.zeros((TILE, width), jnp.float32)

    free = jnp.where(low, depth, 0)

    def gu_copies():
        span = pl.ds(pl.multiple_of(free, depth), depth)
        return (
            pltpu.make_async_copy(dg.at[span], dw_gate, out_sem.at[0]),
            pltpu.make_async_copy(du.at[span], dw_up, out_sem.at[1]),
        )

    def write_gu():
        @pl.loop(0, depth // TILE)
        def _(i):
            there = pl.ds(pl.multiple_of(free + i * TILE, TILE), TILE)
            dg[there, :] = acc1[tile(i), :].astype(jnp.bfloat16)
            du[there, :] = acc2[tile(i), :].astype(jnp.bfloat16)

        for copy in gu_copies():
            copy.start()

    @pl.loop(0, len(END_STEPS))
    def _(t):
        kind = jnp.where(is_end, pick([s[0] for s in END_STEPS], t), pick([s[0] for s in MIDDLE_STEPS], t))
        arg = jnp.where(is_end, pick([s[1] for s in END_STEPS], t), pick([s[1] for s in MIDDLE_STEPS], t))
        pl.when(kind == X)(lambda: x_step(arg))
        for k in range(1, CHIPS):
            pl.when((kind == FORWARD) & (arg == k))(lambda k=k: forward(1, k))
        pl.when(kind == REDUCE)(lambda: reduce_step(arg))
        pl.when(kind == WRITE_GU)(write_gu)
        pl.when(kind == WRITE_DOWN)(write_down)

    for q in range(4):
        down_copy(q).wait()
    for copy in gu_copies():
        copy.wait()
    for slot in range(2 * CHUNKS):
        partner_send(0, 0, slot).wait_send()
    for t in range(2):
        @pl.loop(0, CHIPS)
        def _(chip, t=t):
            for h in range(CHUNKS):
                pl.when(has_above & (chip <= z))(lambda h=h: send(t, 0, chip, h, partner, False).wait_send())
                pl.when(has_below & (chip >= z))(lambda h=h: send(t, 1, chip, h, partner, False).wait_send())
                send(t, 2, chip, h, partner, False).wait_send()


def solution(mesh):
    def step(x, dy, gate, up, w_gate, w_up, w_down):
        rows, depth = x.shape
        tokens, width = gate.shape
        bf16 = jnp.bfloat16
        part = rows // CHUNKS
        hbm = pl.BlockSpec(memory_space=pl.ANY)
        shapes = [
            (rows, depth), (depth, width), (depth, width), (width, depth),
            (tokens, depth), (tokens, depth), (CHIPS, rows, depth), (CHIPS, rows, depth), (CHIPS, rows, depth),
        ]
        dma = pltpu.SemaphoreType.DMA
        out = pl.pallas_call(
            kernel,
            out_shape=[jax.ShapeDtypeStruct(s, bf16) for s in shapes],
            in_specs=[hbm] * 7,
            out_specs=[hbm] * len(shapes),
            scratch_shapes=[
                pltpu.VMEM((depth, width), bf16), pltpu.VMEM((depth, width), bf16), pltpu.VMEM((width, depth), bf16),
                pltpu.VMEM((tokens, width), bf16), pltpu.VMEM((tokens, width), bf16),
                pltpu.VMEM((depth, width), jnp.float32), pltpu.VMEM((depth, width), jnp.float32),
                pltpu.VMEM((2, rows, depth), bf16),
                pltpu.VMEM((2, rows, width), bf16), pltpu.VMEM((2, rows, width), bf16), pltpu.VMEM((rows, width), bf16),
                pltpu.VMEM((2 * CHUNKS, part, depth), bf16),
                dma((3,)), dma, dma((2, 2)), dma((6,)),
                dma((2, 2 * CHIPS, CHUNKS)), dma((2, 3, CHIPS, CHUNKS)),
                dma((CHIPS, CHUNKS)), dma((CHIPS, CHUNKS)), dma((CHIPS, CHUNKS)), dma((2 * CHUNKS,)),
            ],
            compiler_params=pltpu.CompilerParams(collective_id=0, has_side_effects=True, vmem_limit_bytes=67043328),
            cost_estimate=pl.CostEstimate(flops=12 * tokens * depth * width, bytes_accessed=150 * 2**20, transcendentals=0),
        )(x, dy, gate, up, w_gate, w_up, w_down)
        return tuple(out[:4])

    whole, rows, cols = P(("dp", "tp"), None), P("tp", None), P(None, "tp")
    return jax.shard_map(
        step,
        mesh=mesh,
        in_specs=(whole, whole, P("dp", "tp"), P("dp", "tp"), cols, cols, rows),
        out_specs=(whole, P("dp", "tp"), P("dp", "tp"), whole),
        check_vma=False,
    )
```

time: 491 us -> 344 us (0.70)
  Pallas kernels: 0 us -> 327 us
  waiting for transfers between devices: 308 us -> 0 us
  matrix products: 156 us -> 0 us
  between operations: 13.7 us -> 0.65 us
    pallas_call x0 -> x1, Pallas kernels: none -> 327 us  [step(): pl.pallas_call(kernel, out_shape=[jax.ShapeDtypeStruct(s, bf16) for s in...]
    unnamed x5 -> x0, waiting for transfers between devices: 238 us -> none
    dot_general x6 -> x0, matrix products: 156 us -> none  [the longest x3 74.6 us: by_group(): jnp.einsum('gta,gtb->gab', a, b, preferred_element_type=jnp.float32)]
    reshape x1 -> x0, waiting for transfers between devices: 69.9 us -> none  [by_group(): a, b = (t.reshape(groups, -1, t.shape[-1]) for t in (a, b))]
    unnamed x2 -> x10, local copies, waits for them, and re-layouts: 12.8 us -> 12.7 us
  transfers between devices with their start and end apart: 3 -> 0, of which waited for: 3 -> 0; matrix products, arithmetic and copies ran while one was open for 34% -> 0% of each run, Pallas kernels for 0% -> 0%
where the time goes in v1:
time: 344 us; the launch traced here: 340 us
  Pallas kernels  327 us (95%)
  local copies, waits for them, and re-layouts  12.7 us (4%)
    pallas_call x1, Pallas kernels, step(): pl.pallas_call(kernel, out_shape=[jax.ShapeDtypeStruct(s, bf16) for s in...  327 us
    unnamed x10, local copies, waits for them, and re-layouts  12.7 us

profile of v1, /device:TPU:0, one launch (start us, length us, event | category | flops | bytes accessed | tf_op | source)
XLA Modules:
  0.0 340.3 jit_solution(16840407578853866788)
XLA Ops:
  0.6 326.9 %shard_map.102 = (bf16[512,2048]{1,0:T(8,128)(2,1)}, bf16[2048,1024]{1,0:T(8,128)(2,1)}, bf16[2048,1024]{1,0:T(8,128)(2,1)}, bf16[1024,2048]{1,0:T(8,128)(2,1)},...) custom-call(bf16[512,2048]{1,0:T(8,128)(2,1)} %x.1, ...), custom_call_target="tpu_custom_call" | custom-call | flops 103079215104 | bytes 157286400 | tf_op jit(solution)/shard_map/pallas_call | solution.py:379
  327.6 0.0 copy-start.2
  327.6 3.3 copy.15
  330.9 0.0 copy-done.2
  330.9 0.0 copy-start.1
  330.9 2.1 copy.16
  333.0 1.6 copy-done.1
  334.6 0.0 copy-start
  334.6 2.1 copy.17
  336.7 1.6 copy-done
  338.3 2.0 copy.18
Async XLA Ops:
  327.6 3.3 copy-start.2
  330.9 3.7 %copy-start.1 = (bf16[2048,1024]{1,0:T(8,128)(2,1)S(1)}, bf16[2048,1024]{1,0:T(8,128)(2,1)}, u32[]{:S(2)}) copy-start(bf16[2048,1024]{1,0:T(8,128)(2,1)} %get-tuple-element.18) | copy-start | bytes 12582916
  334.6 3.7 %copy-start = (bf16[1024,2048]{1,0:T(8,128)(2,1)S(1)}, bf16[1024,2048]{1,0:T(8,128)(2,1)}, u32[]{:S(2)}) copy-start(bf16[1024,2048]{1,0:T(8,128)(2,1)} %get-tuple-element.19) | copy-start | bytes 12582916

commit v2 on v1

--- a/solution.py
+++ b/solution.py
@@ -9,18 +9,19 @@
 
 MESH = pl.DeviceIdType.MESH
 CHUNKS = 2
+PIECES = 2
 TILE = 256
 CHIPS = 4
 NT = (((1,), (1,)), ((), ()))
 TN = (((0,), (0,)), ((), ()))
-X, FORWARD, REDUCE, WRITE_GU, WRITE_DOWN = range(5)
+X, FORWARD, REDUCE, WRITE_GU, WRITE_DOWN, OWN, FINISH = range(7)
 END_STEPS = (
     (REDUCE, 0), (REDUCE, 1), (WRITE_DOWN, 0), (X, 0), (X, 1), (FORWARD, 1), (X, 2), (X, 3), (REDUCE, 2),
-    (FORWARD, 2), (X, 4), (X, 5), (FORWARD, 3), (X, 6), (X, 7), (WRITE_GU, 0), (REDUCE, 3),
+    (FORWARD, 2), (X, 4), (X, 5), (FORWARD, 3), (X, 6), (X, 7), (WRITE_GU, 0), (OWN, 0), (FINISH, 0),
 )
 MIDDLE_STEPS = (
     (WRITE_DOWN, 0), (X, 0), (X, 1), (FORWARD, 1), (X, 2), (X, 3), (X, 4), (X, 5), (FORWARD, 2),
-    (X, 6), (X, 7), (FORWARD, 3), (REDUCE, 0), (REDUCE, 1), (REDUCE, 2), (WRITE_GU, 0), (REDUCE, 3),
+    (X, 6), (X, 7), (FORWARD, 3), (REDUCE, 0), (REDUCE, 1), (REDUCE, 2), (WRITE_GU, 0), (OWN, 0), (FINISH, 0),
 )
 
 
@@ -35,11 +36,16 @@
     return lax.dot_general(a, b, dims, preferred_element_type=jnp.float32)
 
 
+def free_rows(depth):
+    z = lax.axis_index("tp") // 2
+    return pl.multiple_of(jnp.where(z < CHIPS // 2, depth, 0), depth)
+
+
 def kernel(
     x, dy, gate, up, w_gate, w_up, w_down,
-    dx, dw_gate, dw_up, dw_down, dy_all, x_all, from_partner, from_below, from_above,
-    wg, wu, wd, dg, du, acc1, acc2, tok, gv, uv, hid, st,
-    w_sem, tok_sem, gate_sem, out_sem, recv_sem, send_sem, partner_sem, below_sem, above_sem, st_sem,
+    dx, dg, du, wd, dy_all, x_all, from_partner, from_below, from_above,
+    wg, wu, acc1, acc2, tok, gv, uv, hid, st, terms,
+    w_sem, tok_sem, gate_sem, recv_sem, send_sem, partner_sem, below_sem, above_sem, st_sem,
 ):
     rows, depth = x.shape
     width = gate.shape[1]
@@ -154,7 +160,7 @@
     for copy in weights:
         copy.wait()
 
-    def take_tokens(t, s, b, slot):
+    def take_tokens(t, s, b):
         @pl.when(lax.rem(s, 2) == 1)
         def _():
             for h in range(CHUNKS):
@@ -162,13 +168,13 @@
 
         @pl.when(s == 0)
         def _():
-            pltpu.make_async_copy(own[t], tok.at[slot], tok_sem).start()
+            pltpu.make_async_copy(own[t], tok, tok_sem).start()
 
         @pl.when(s > 0)
         def _():
-            pltpu.make_async_copy(whole[t].at[block_rows(b)], tok.at[slot], tok_sem).start()
-
-        pltpu.make_async_copy(own[t], tok.at[slot], tok_sem).wait()
+            pltpu.make_async_copy(whole[t].at[block_rows(b)], tok, tok_sem).start()
+
+        pltpu.make_async_copy(own[t], tok, tok_sem).wait()
 
     def partner_send(chip, h, slot):
         return pltpu.make_async_remote_copy(
@@ -193,7 +199,7 @@
                 forward(0, j)
                 send_x_after(j)
 
-        take_tokens(0, s, b, slot)
+        take_tokens(0, s, b)
 
         @pl.when(s + 1 < 2 * CHIPS)
         def _():
@@ -206,7 +212,7 @@
         @pl.loop(0, width // TILE)
         def _(i):
             cols = tile(i)
-            d_hidden = dot(tok[slot], wd[cols, :], NT)
+            d_hidden = dot(tok[...], wd[cols, :], NT)
             g = gv[slot, :, cols].astype(jnp.float32)
             u = uv[slot, :, cols].astype(jnp.float32)
             s_ = jax.nn.sigmoid(g)
@@ -218,8 +224,8 @@
         @pl.loop(0, width // TILE)
         def _(i):
             left = hid[:, tile(i)]
-            acc1[tile(i), :] += dot(left, tok[slot, :, :width], TN)
-            acc1[pl.ds(pl.multiple_of(width + i * TILE, TILE), TILE), :] += dot(left, tok[slot, :, width:], TN)
+            acc1[tile(i), :] += dot(left, tok[:, :width], TN)
+            acc1[pl.ds(pl.multiple_of(width + i * TILE, TILE), TILE), :] += dot(left, tok[:, width:], TN)
 
         @pl.when(odd == 1)
         def _():
@@ -242,23 +248,32 @@
     def x_step(s):
         chip = arrival(s // 2)
         b = 2 * chip + jnp.where(lax.rem(s, 2) == 0, c, other)
-        slot = lax.rem(s, 2)
-        take_tokens(1, s, b, slot)
+        take_tokens(1, s, b)
 
         @pl.loop(0, depth // TILE)
         def _(i):
-            left = tok[slot, :, tile(i)]
+            left = tok[:, tile(i)]
             acc1[tile(i), :] += dot(left, dg[block_rows(b), :], TN)
             acc2[tile(i), :] += dot(left, du[block_rows(b), :], TN)
 
-    def incoming(buffer, sem, chip, h, j):
-        piece = buffer.at[chip, tile(h, part)]
+    fine = part // PIECES
+
+    def arrived(buffer, sem, chip, at, size):
+        piece = buffer.at[chip, pl.ds(pl.multiple_of(at * size, size), size)]
         pltpu.make_async_remote_copy(
-            src_ref=piece, dst_ref=piece, send_sem=st_sem.at[0], recv_sem=sem.at[chip, h], device_id=partner, device_id_type=MESH
+            src_ref=piece, dst_ref=piece, send_sem=st_sem.at[0], recv_sem=sem.at[chip, at], device_id=partner, device_id_type=MESH
         ).wait_recv()
-        copy = pltpu.make_async_copy(piece, wd.at[pl.ds(j * part, part)], tok_sem)
+
+    def take_term(buffer, chip, at, size, j):
+        copy = pltpu.make_async_copy(
+            buffer.at[chip, pl.ds(pl.multiple_of(at * size, size), size)], terms.at[j, pl.ds(0, size)], tok_sem
+        )
         copy.start()
         copy.wait()
+
+    def own_term(b, h, i):
+        here = chunk_rows(b, h)
+        return dot(dg[here, :], wg[tile(i), :], NT) + dot(du[here, :], wu[tile(i), :], NT)
 
     def reduce_step(r):
         chip = target(r)
@@ -268,75 +283,91 @@
         def _(h):
             slot = 2 * lax.rem(r, 2) + h
             partner_send(chip, 0, slot).wait_send()
-            incoming(from_partner, partner_sem, chip, h, 0)
-            use_below, use_above = (chip >= z) & has_below, (chip <= z) & has_above
-            for j, (use, buffer, sem) in enumerate(((use_below, from_below, below_sem), (use_above, from_above, above_sem)), 1):
-                pl.when(use)(lambda j=j, buffer=buffer, sem=sem: incoming(buffer, sem, chip, h, j))
-
-                @pl.when(jnp.logical_not(use))
-                def _(j=j):
-                    wd[j * part:(j + 1) * part, :] = jnp.zeros((part, depth), jnp.bfloat16)
+            arrived(from_partner, partner_sem, chip, h, part)
+            take_term(from_partner, chip, h, part, 0)
+            going_up = chip > z
+            for use, buffer, sem in (
+                (going_up & has_below, from_below, below_sem),
+                (jnp.logical_not(going_up) & has_above, from_above, above_sem),
+            ):
+                @pl.when(use)
+                def _(buffer=buffer, sem=sem):
+                    for q in range(PIECES):
+                        arrived(buffer, sem, chip, PIECES * h + q, fine)
+                    take_term(buffer, chip, h, part, 1)
+
+            @pl.when(is_end)
+            def _():
+                terms[1] = jnp.zeros((part, depth), jnp.bfloat16)
 
             @pl.loop(0, depth // TILE)
             def _(i):
-                here = chunk_rows(b, h)
-                total = dot(dg[here, :], wg[tile(i), :], NT) + dot(du[here, :], wu[tile(i), :], NT)
-                for j in range(3):
-                    total += wd[j * part:(j + 1) * part, tile(i)].astype(jnp.float32)
+                total = own_term(b, h, i)
+                for j in range(2):
+                    total += terms[j, :, tile(i)].astype(jnp.float32)
                 st[slot, :, tile(i)] = total.astype(jnp.bfloat16)
 
             def pass_on(buffer, sem, device):
-                pltpu.make_async_remote_copy(
-                    src_ref=st.at[slot],
-                    dst_ref=buffer.at[chip, tile(h, part)],
-                    send_sem=st_sem.at[slot],
-                    recv_sem=sem.at[chip, h],
-                    device_id=device,
-                    device_id_type=MESH,
-                ).start()
-
-            pl.when(chip > z)(lambda: pass_on(from_below, below_sem, above))
-            pl.when(chip < z)(lambda: pass_on(from_above, above_sem, below))
-            pl.when(chip == z)(lambda: pltpu.make_async_copy(st.at[slot], dx.at[tile(h, part)], st_sem.at[slot]).start())
-
-    half = depth // 2
-    stage = [gv.at[0], gv.at[1], uv.at[0], uv.at[1]]
-
-    def down_copy(q):
-        span = width // 2
-        return pltpu.make_async_copy(
-            stage[q], dw_down.at[pl.ds((q % 2) * span, span), pl.ds((q // 2) * width, width)], out_sem.at[2 + q]
-        )
+                for q in range(PIECES):
+                    at = PIECES * h + q
+                    pltpu.make_async_remote_copy(
+                        src_ref=st.at[slot, pl.ds(q * fine, fine)],
+                        dst_ref=buffer.at[chip, pl.ds(pl.multiple_of(at * fine, fine), fine)],
+                        send_sem=st_sem.at[slot],
+                        recv_sem=sem.at[chip, at],
+                        device_id=device,
+                        device_id_type=MESH,
+                    ).start()
+
+            pl.when(going_up)(lambda: pass_on(from_below, below_sem, above))
+            pl.when(jnp.logical_not(going_up))(lambda: pass_on(from_above, above_sem, below))
+
+    def halves(i):
+        return lax.rem(i, width // TILE), (i // (width // TILE)) * rows
+
+    def own_step():
+        @pl.loop(0, CHUNKS)
+        def _(h):
+            arrived(from_partner, partner_sem, z, h, part)
+            take_term(from_partner, z, h, part, 0)
+
+            @pl.loop(0, depth // TILE)
+            def _(i):
+                column, down = halves(i)
+                total = own_term(me, h, i) + terms[0, :, tile(i)].astype(jnp.float32)
+                acc1[pl.ds(pl.multiple_of(down + h * part, part), part), tile(column)] = total
+
+    def finish():
+        for at in range(CHUNKS * PIECES):
+            for j, (use, buffer, sem) in enumerate(((has_below, from_below, below_sem), (has_above, from_above, above_sem))):
+                @pl.when(use)
+                def _(j=j, buffer=buffer, sem=sem):
+                    arrived(buffer, sem, z, at, fine)
+                    take_term(buffer, z, at, fine, j)
+                    for side in range(2):
+                        here = pl.ds(side * rows + at * fine, fine)
+                        acc1[here, :] += terms[j, :fine, side * width:(side + 1) * width].astype(jnp.float32)
+            for side in range(2):
+                here = pl.ds(side * rows + at * fine, fine)
+                dx[at * fine:(at + 1) * fine, side * width:(side + 1) * width] = acc1[here, :].astype(jnp.bfloat16)
 
     def write_down():
-        for q in range(4):
-            span = width // 2
-            stage[q][...] = acc1[q * span:(q + 1) * span, :].astype(jnp.bfloat16)
-            down_copy(q).start()
+        for side in range(2):
+            wd[:, side * width:(side + 1) * width] = acc1[side * width:(side + 1) * width, :].astype(jnp.bfloat16)
 
         @pl.loop(0, depth // TILE)
         def _(i):
             acc1[tile(i), :] = jnp.zeros((TILE, width), jnp.float32)
             acc2[tile(i), :] = jnp.zeros((TILE, width), jnp.float32)
 
-    free = jnp.where(low, depth, 0)
-
-    def gu_copies():
-        span = pl.ds(pl.multiple_of(free, depth), depth)
-        return (
-            pltpu.make_async_copy(dg.at[span], dw_gate, out_sem.at[0]),
-            pltpu.make_async_copy(du.at[span], dw_up, out_sem.at[1]),
-        )
-
     def write_gu():
+        free = free_rows(depth)
+
         @pl.loop(0, depth // TILE)
         def _(i):
             there = pl.ds(pl.multiple_of(free + i * TILE, TILE), TILE)
             dg[there, :] = acc1[tile(i), :].astype(jnp.bfloat16)
             du[there, :] = acc2[tile(i), :].astype(jnp.bfloat16)
-
-        for copy in gu_copies():
-            copy.start()
 
     @pl.loop(0, len(END_STEPS))
     def _(t):
@@ -348,11 +379,9 @@
         pl.when(kind == REDUCE)(lambda: reduce_step(arg))
         pl.when(kind == WRITE_GU)(write_gu)
         pl.when(kind == WRITE_DOWN)(write_down)
-
-    for q in range(4):
-        down_copy(q).wait()
-    for copy in gu_copies():
-        copy.wait()
+        pl.when(kind == OWN)(own_step)
+        pl.when(kind == FINISH)(finish)
+
     for slot in range(2 * CHUNKS):
         partner_send(0, 0, slot).wait_send()
     for t in range(2):
@@ -364,38 +393,55 @@
                 send(t, 2, chip, h, partner, False).wait_send()
 
 
+def put_out(dx, dg, du, dwd, dx_out, dw_gate, dw_up, dw_down, sems):
+    depth = dw_gate.shape[0]
+    free = pl.ds(free_rows(depth), depth)
+    copies = [
+        pltpu.make_async_copy(src, dst, sems.at[i])
+        for i, (src, dst) in enumerate(((dg.at[free], dw_gate), (du.at[free], dw_up), (dwd, dw_down), (dx, dx_out)))
+    ]
+    for copy in copies:
+        copy.start()
+    for copy in copies:
+        copy.wait()
+
+
 def solution(mesh):
     def step(x, dy, gate, up, w_gate, w_up, w_down):
         rows, depth = x.shape
         tokens, width = gate.shape
         bf16 = jnp.bfloat16
         part = rows // CHUNKS
-        hbm = pl.BlockSpec(memory_space=pl.ANY)
-        shapes = [
-            (rows, depth), (depth, width), (depth, width), (width, depth),
-            (tokens, depth), (tokens, depth), (CHIPS, rows, depth), (CHIPS, rows, depth), (CHIPS, rows, depth),
-        ]
+        hbm, vmem = pl.BlockSpec(memory_space=pl.ANY), pl.BlockSpec(memory_space=pltpu.VMEM)
+        held = [(rows, depth), (tokens, width), (tokens, width), (width, depth)]
+        gathered = [(tokens, depth), (tokens, depth), (CHIPS, rows, depth), (CHIPS, rows, depth), (CHIPS, rows, depth)]
         dma = pltpu.SemaphoreType.DMA
-        out = pl.pallas_call(
+        held_out = pl.pallas_call(
             kernel,
-            out_shape=[jax.ShapeDtypeStruct(s, bf16) for s in shapes],
+            out_shape=[pltpu.VMEM(s, bf16) for s in held] + [jax.ShapeDtypeStruct(s, bf16) for s in gathered],
             in_specs=[hbm] * 7,
-            out_specs=[hbm] * len(shapes),
+            out_specs=[vmem] * len(held) + [hbm] * len(gathered),
             scratch_shapes=[
-                pltpu.VMEM((depth, width), bf16), pltpu.VMEM((depth, width), bf16), pltpu.VMEM((width, depth), bf16),
-                pltpu.VMEM((tokens, width), bf16), pltpu.VMEM((tokens, width), bf16),
+                pltpu.VMEM((depth, width), bf16), pltpu.VMEM((depth, width), bf16),
                 pltpu.VMEM((depth, width), jnp.float32), pltpu.VMEM((depth, width), jnp.float32),
-                pltpu.VMEM((2, rows, depth), bf16),
+                pltpu.VMEM((rows, depth), bf16),
                 pltpu.VMEM((2, rows, width), bf16), pltpu.VMEM((2, rows, width), bf16), pltpu.VMEM((rows, width), bf16),
-                pltpu.VMEM((2 * CHUNKS, part, depth), bf16),
-                dma((3,)), dma, dma((2, 2)), dma((6,)),
+                pltpu.VMEM((2 * CHUNKS, part, depth), bf16), pltpu.VMEM((2, part, depth), bf16),
+                dma((3,)), dma, dma((2, 2)),
                 dma((2, 2 * CHIPS, CHUNKS)), dma((2, 3, CHIPS, CHUNKS)),
-                dma((CHIPS, CHUNKS)), dma((CHIPS, CHUNKS)), dma((CHIPS, CHUNKS)), dma((2 * CHUNKS,)),
+                dma((CHIPS, CHUNKS)), dma((CHIPS, CHUNKS * PIECES)), dma((CHIPS, CHUNKS * PIECES)), dma((2 * CHUNKS,)),
             ],
-            compiler_params=pltpu.CompilerParams(collective_id=0, has_side_effects=True, vmem_limit_bytes=67043328),
+            compiler_params=pltpu.CompilerParams(collective_id=0, has_side_effects=True, vmem_limit_bytes=41 * 2**20),
             cost_estimate=pl.CostEstimate(flops=12 * tokens * depth * width, bytes_accessed=150 * 2**20, transcendentals=0),
-        )(x, dy, gate, up, w_gate, w_up, w_down)
-        return tuple(out[:4])
+        )(x, dy, gate, up, w_gate, w_up, w_down)[: len(held)]
+        return pl.pallas_call(
+            put_out,
+            out_shape=[jax.ShapeDtypeStruct(s, bf16) for s in ((rows, depth), (depth, width), (depth, width), (width, depth))],
+            in_specs=[vmem] * len(held),
+            out_specs=[hbm] * 4,
+            scratch_shapes=[dma((4,))],
+            compiler_params=pltpu.CompilerParams(vmem_limit_bytes=2**20),
+        )(*held_out)
 
     whole, rows, cols = P(("dp", "tp"), None), P("tp", None), P(None, "tp")
     return jax.shard_map(

time: 344 us -> 332 us (0.965)
  local copies, waits for them, and re-layouts: 12.7 us -> 0 us
    unnamed x10 -> x0, local copies, waits for them, and re-layouts: 12.7 us -> none
    pallas_call x1 -> x2, Pallas kernels: 327 us -> 327 us  [the longest x1 322 us: step(): pl.pallas_call(kernel, out_shape=[pltpu.VMEM(s, bf16) for s in held] + [j...]
where the time goes in v2:
time: 332 us; the launch traced here: 328 us
  Pallas kernels  327 us (98%)
    pallas_call x1, Pallas kernels, step(): pl.pallas_call(kernel, out_shape=[pltpu.VMEM(s, bf16) for s in held] + [j...  322 us

profile of v2, /device:TPU:0, one launch (start us, length us, event | category | flops | bytes accessed | tf_op | source)
XLA Modules:
  0.0 328.1 jit_solution(4922425683430656690)
XLA Ops:
  0.6 322.2 %shard_map.102 = (bf16[512,2048]{1,0:T(8,128)(2,1)S(1)}, bf16[4096,1024]{1,0:T(8,128)(2,1)S(1)}, bf16[4096,1024]{1,0:T(8,128)(2,1)S(1)}, bf16[1024,2048]{1,0:T(8...) custom-call(bf16[512,2048]{1,0:T(8,128)(2,1)} %x.1, ...), custom_call_target="tpu_custom_call" | custom-call | flops 103079215104 | bytes 157286400 | tf_op jit(solution)/shard_map/pallas_call | solution.py:419
  322.8 5.3 %shard_map.103 = (bf16[512,2048]{1,0:T(8,128)(2,1)}, bf16[2048,1024]{1,0:T(8,128)(2,1)}, bf16[2048,1024]{1,0:T(8,128)(2,1)}, bf16[1024,2048]{1,0:T(8,128)(2,1)}) custom-call(bf16[512,2048]{1,0:T(8,128)(2,1)S(1)} %get-tuple-element.8.dx, bf16[4096,1024]{1,0:T(8,128)(2,1)S(1)} %get-tuple-element.9.dg, bf16[4096,1024]{1,0:T(8,128)(2,1)S(1)} %get-tuple-element.10.du, ...), custom_call_target="tpu_custom_call" | custom-call | tf_op jit(solution)/shard_map/pallas_call | solution.py:437

commit v3 on v2

--- a/solution.py
+++ b/solution.py
@@ -77,12 +77,12 @@
     def tile(i, size=TILE):
         return pl.ds(pl.multiple_of(i * size, size), size)
 
-    own = (dy, x)
+    own = ([st.at[CHUNKS + h] for h in range(CHUNKS)], [x.at[pl.ds(h * part, part)] for h in range(CHUNKS)])
     whole = (dy_all, x_all)
 
     def send(t, way, chip, h, device, mine):
         b = 2 * chip + c
-        src = own[t].at[pl.ds(h * part, part)] if mine else whole[t].at[chunk_rows(b, h)]
+        src = own[t][h] if mine else whole[t].at[chunk_rows(b, h)]
         return pltpu.make_async_remote_copy(
             src_ref=src,
             dst_ref=whole[t].at[chunk_rows(b, h)],
@@ -102,39 +102,49 @@
             device_id_type=MESH,
         ).wait_recv()
 
-    def send_own(t, ways):
+    def send_own(t, ways, before=None):
         for h in range(CHUNKS):
+            if before is not None:
+                before[h].wait()
             for way, device in enumerate((above, below, partner)):
                 if ways[way] is True:
                     send(t, way, z, h, device, True).start()
                 elif ways[way] is not False:
                     pl.when(ways[way])(lambda t=t, way=way, h=h, device=device: send(t, way, z, h, device, True).start())
 
-    def forward(t, k):
+    def forward(t, k, from_below=True, from_above=True):
         for h in range(CHUNKS):
-            @pl.when(z - k >= 0)
+            @pl.when((z - k >= 0) & from_below)
             def _():
                 chip = z - k
                 await_chunk(t, 2 * chip + c, h)
                 pl.when(has_above)(lambda: send(t, 0, chip, h, above, False).start())
                 send(t, 2, chip, h, partner, False).start()
 
-            @pl.when(z + k <= last)
+            @pl.when((z + k <= last) & from_above)
             def _():
                 chip = z + k
                 await_chunk(t, 2 * chip + c, h)
                 pl.when(has_below)(lambda: send(t, 1, chip, h, below, False).start())
                 send(t, 2, chip, h, partner, False).start()
 
+    def sent(t, chip, h):
+        pl.when(has_above & (chip <= z))(lambda: send(t, 0, chip, h, partner, False).wait_send())
+        pl.when(has_below & (chip >= z))(lambda: send(t, 1, chip, h, partner, False).wait_send())
+        send(t, 2, chip, h, partner, False).wait_send()
+
     def send_x_after(k):
         send_own(1, (has_above & (z == k), has_below & (last - z == k), False))
 
+    mine = [pltpu.make_async_copy(dy.at[pl.ds(h * part, part)], own[0][h], w_sem.at[3 + h]) for h in range(CHUNKS)]
+    for copy in mine:
+        copy.start()
     barrier = pltpu.get_barrier_semaphore()
     pl.semaphore_signal(barrier, inc=1, device_id=partner, device_id_type=MESH)
     pl.when(has_below)(lambda: pl.semaphore_signal(barrier, inc=1, device_id=below, device_id_type=MESH))
     pl.when(has_above)(lambda: pl.semaphore_signal(barrier, inc=1, device_id=above, device_id_type=MESH))
     pl.semaphore_wait(barrier, jnp.where(is_end, 2, 3))
-    send_own(0, (has_above, has_below, True))
+    send_own(0, (has_above, has_below, True), mine)
     send_x_after(0)
     send_own(1, (False, False, True))
 
@@ -168,13 +178,13 @@
 
         @pl.when(s == 0)
         def _():
-            pltpu.make_async_copy(own[t], tok, tok_sem).start()
+            pltpu.make_async_copy((dy, x)[t], tok, tok_sem).start()
 
         @pl.when(s > 0)
         def _():
             pltpu.make_async_copy(whole[t].at[block_rows(b)], tok, tok_sem).start()
 
-        pltpu.make_async_copy(own[t], tok, tok_sem).wait()
+        pltpu.make_async_copy((dy, x)[t], tok, tok_sem).wait()
 
     def partner_send(chip, h, slot):
         return pltpu.make_async_remote_copy(
@@ -198,6 +208,8 @@
             def _(j=j):
                 forward(0, j)
                 send_x_after(j)
+                if j == CHIPS - 1:
+                    forward(1, 1, z == 1, z == last - 1)
 
         take_tokens(0, s, b)
 
@@ -230,6 +242,11 @@
         @pl.when(odd == 1)
         def _():
             base = 2 * lax.rem(k, 2)
+
+            @pl.when(k == 1)
+            def _():
+                for h in range(CHUNKS):
+                    sent(0, z, h)
 
             @pl.when(k >= 2)
             def _():
@@ -337,6 +354,12 @@
                 total = own_term(me, h, i) + terms[0, :, tile(i)].astype(jnp.float32)
                 acc1[pl.ds(pl.multiple_of(down + h * part, part), part), tile(column)] = total
 
+        @pl.loop(0, CHIPS)
+        def _(chip):
+            for h in range(CHUNKS):
+                pl.when(chip != z)(lambda h=h: sent(0, chip, h))
+                sent(1, chip, h)
+
     def finish():
         for at in range(CHUNKS * PIECES):
             for j, (use, buffer, sem) in enumerate(((has_below, from_below, below_sem), (has_above, from_above, above_sem))):
@@ -374,7 +397,8 @@
         kind = jnp.where(is_end, pick([s[0] for s in END_STEPS], t), pick([s[0] for s in MIDDLE_STEPS], t))
         arg = jnp.where(is_end, pick([s[1] for s in END_STEPS], t), pick([s[1] for s in MIDDLE_STEPS], t))
         pl.when(kind == X)(lambda: x_step(arg))
-        for k in range(1, CHIPS):
+        pl.when((kind == FORWARD) & (arg == 1))(lambda: forward(1, 1, z != 1, z != last - 1))
+        for k in range(2, CHIPS):
             pl.when((kind == FORWARD) & (arg == k))(lambda k=k: forward(1, k))
         pl.when(kind == REDUCE)(lambda: reduce_step(arg))
         pl.when(kind == WRITE_GU)(write_gu)
@@ -384,13 +408,6 @@
 
     for slot in range(2 * CHUNKS):
         partner_send(0, 0, slot).wait_send()
-    for t in range(2):
-        @pl.loop(0, CHIPS)
-        def _(chip, t=t):
-            for h in range(CHUNKS):
-                pl.when(has_above & (chip <= z))(lambda h=h: send(t, 0, chip, h, partner, False).wait_send())
-                pl.when(has_below & (chip >= z))(lambda h=h: send(t, 1, chip, h, partner, False).wait_send())
-                send(t, 2, chip, h, partner, False).wait_send()
 
 
 def put_out(dx, dg, du, dwd, dx_out, dw_gate, dw_up, dw_down, sems):
@@ -427,7 +444,7 @@
                 pltpu.VMEM((rows, depth), bf16),
                 pltpu.VMEM((2, rows, width), bf16), pltpu.VMEM((2, rows, width), bf16), pltpu.VMEM((rows, width), bf16),
                 pltpu.VMEM((2 * CHUNKS, part, depth), bf16), pltpu.VMEM((2, part, depth), bf16),
-                dma((3,)), dma, dma((2, 2)),
+                dma((3 + CHUNKS,)), dma, dma((2, 2)),
                 dma((2, 2 * CHIPS, CHUNKS)), dma((2, 3, CHIPS, CHUNKS)),
                 dma((CHIPS, CHUNKS)), dma((CHIPS, CHUNKS * PIECES)), dma((CHIPS, CHUNKS * PIECES)), dma((2 * CHUNKS,)),
             ],

time: 332 us -> 330 us (level)
  no operation moved by 1% of the time
where the time goes in v3:
time: 330 us; the launch traced here: 328 us
  Pallas kernels  327 us (99%)
    pallas_call x1, Pallas kernels, step(): pl.pallas_call(kernel, out_shape=[pltpu.VMEM(s, bf16) for s in held] + [j...  322 us

profile of v3, /device:TPU:0, one launch (start us, length us, event | category | flops | bytes accessed | tf_op | source)
XLA Modules:
  0.0 328.0 jit_solution(9503046640722777934)
XLA Ops:
  0.6 322.1 %shard_map.102 = (bf16[512,2048]{1,0:T(8,128)(2,1)S(1)}, bf16[4096,1024]{1,0:T(8,128)(2,1)S(1)}, bf16[4096,1024]{1,0:T(8,128)(2,1)S(1)}, bf16[1024,2048]{1,0:T(8...) custom-call(bf16[512,2048]{1,0:T(8,128)(2,1)} %x.1, ...), custom_call_target="tpu_custom_call" | custom-call | flops 103079215104 | bytes 157286400 | tf_op jit(solution)/shard_map/pallas_call | solution.py:436
  322.7 5.3 %shard_map.103 = (bf16[512,2048]{1,0:T(8,128)(2,1)}, bf16[2048,1024]{1,0:T(8,128)(2,1)}, bf16[2048,1024]{1,0:T(8,128)(2,1)}, bf16[1024,2048]{1,0:T(8,128)(2,1)}) custom-call(bf16[512,2048]{1,0:T(8,128)(2,1)S(1)} %get-tuple-element.8.dx, bf16[4096,1024]{1,0:T(8,128)(2,1)S(1)} %get-tuple-element.9.dg, bf16[4096,1024]{1,0:T(8,128)(2,1)S(1)} %get-tuple-element.10.du, ...), custom_call_target="tpu_custom_call" | custom-call | tf_op jit(solution)/shard_map/pallas_call | solution.py:454

commit v4 on v3

--- a/solution.py
+++ b/solution.py
@@ -43,7 +43,7 @@
 
 def kernel(
     x, dy, gate, up, w_gate, w_up, w_down,
-    dx, dg, du, wd, dy_all, x_all, from_partner, from_below, from_above,
+    dx, dg, du, wd, last_own, last_below, last_above, dy_all, x_all, from_partner, from_below, from_above,
     wg, wu, acc1, acc2, tok, gv, uv, hid, st, terms,
     w_sem, tok_sem, gate_sem, recv_sem, send_sem, partner_sem, below_sem, above_sem, st_sem,
 ):
@@ -324,20 +324,30 @@
                     total += terms[j, :, tile(i)].astype(jnp.float32)
                 st[slot, :, tile(i)] = total.astype(jnp.bfloat16)
 
-            def pass_on(buffer, sem, device):
+            def pass_on(buffer, sem, device, landing, is_final):
                 for q in range(PIECES):
                     at = PIECES * h + q
-                    pltpu.make_async_remote_copy(
-                        src_ref=st.at[slot, pl.ds(q * fine, fine)],
-                        dst_ref=buffer.at[chip, pl.ds(pl.multiple_of(at * fine, fine), fine)],
-                        send_sem=st_sem.at[slot],
-                        recv_sem=sem.at[chip, at],
-                        device_id=device,
-                        device_id_type=MESH,
-                    ).start()
-
-            pl.when(going_up)(lambda: pass_on(from_below, below_sem, above))
-            pl.when(jnp.logical_not(going_up))(lambda: pass_on(from_above, above_sem, below))
+
+                    def start(dst, q=q, at=at):
+                        pltpu.make_async_remote_copy(
+                            src_ref=st.at[slot, pl.ds(q * fine, fine)],
+                            dst_ref=dst,
+                            send_sem=st_sem.at[slot],
+                            recv_sem=sem.at[chip, at],
+                            device_id=device,
+                            device_id_type=MESH,
+                        ).start()
+
+                    piece = buffer.at[chip, pl.ds(pl.multiple_of(at * fine, fine), fine)]
+                    if q < PIECES - 1:
+                        start(piece)
+                    else:
+                        to_vmem = is_final & (h == CHUNKS - 1)
+                        pl.when(to_vmem)(lambda start=start: start(landing))
+                        pl.when(jnp.logical_not(to_vmem))(lambda start=start, piece=piece: start(piece))
+
+            pl.when(going_up)(lambda: pass_on(from_below, below_sem, above, last_below, chip == z + 1))
+            pl.when(jnp.logical_not(going_up))(lambda: pass_on(from_above, above_sem, below, last_above, chip == z - 1))
 
     def halves(i):
         return lax.rem(i, width // TILE), (i // (width // TILE)) * rows
@@ -361,8 +371,12 @@
                 sent(1, chip, h)
 
     def finish():
-        for at in range(CHUNKS * PIECES):
-            for j, (use, buffer, sem) in enumerate(((has_below, from_below, below_sem), (has_above, from_above, above_sem))):
+        pieces = CHUNKS * PIECES
+        sides = ((has_below, from_below, below_sem, last_below), (has_above, from_above, above_sem, last_above))
+        for side in range(2):
+            last_own[:, side * width:(side + 1) * width] = acc1[pl.ds(side * rows + (pieces - 1) * fine, fine), :]
+        for at in range(pieces - 1):
+            for j, (use, buffer, sem, _) in enumerate(sides):
                 @pl.when(use)
                 def _(j=j, buffer=buffer, sem=sem):
                     arrived(buffer, sem, z, at, fine)
@@ -373,6 +387,13 @@
             for side in range(2):
                 here = pl.ds(side * rows + at * fine, fine)
                 dx[at * fine:(at + 1) * fine, side * width:(side + 1) * width] = acc1[here, :].astype(jnp.bfloat16)
+        for use, _, sem, landing in sides:
+            pl.when(use)(
+                lambda sem=sem, landing=landing: pltpu.make_async_remote_copy(
+                    src_ref=landing, dst_ref=landing, send_sem=st_sem.at[0], recv_sem=sem.at[z, pieces - 1],
+                    device_id=partner, device_id_type=MESH,
+                ).wait_recv()
+            )
 
     def write_down():
         for side in range(2):
@@ -410,15 +431,31 @@
         partner_send(0, 0, slot).wait_send()
 
 
-def put_out(dx, dg, du, dwd, dx_out, dw_gate, dw_up, dw_down, sems):
+def put_out(dx, dg, du, dwd, last_own, last_below, last_above, dx_out, dw_gate, dw_up, dw_down, last, sems):
     depth = dw_gate.shape[0]
+    head = dx.shape[0] - last.shape[0]
+    z = lax.axis_index("tp") // 2
     free = pl.ds(free_rows(depth), depth)
-    copies = [
-        pltpu.make_async_copy(src, dst, sems.at[i])
-        for i, (src, dst) in enumerate(((dg.at[free], dw_gate), (du.at[free], dw_up), (dwd, dw_down), (dx, dx_out)))
-    ]
-    for copy in copies:
+    pairs = (
+        (dg.at[free], dw_gate), (du.at[free], dw_up), (dwd, dw_down),
+        (dx.at[:head], dx_out.at[:head]), (last, dx_out.at[head:]),
+    )
+    copies = [pltpu.make_async_copy(src, dst, sems.at[i]) for i, (src, dst) in enumerate(pairs)]
+    for copy in copies[:-1]:
         copy.start()
+    for case, terms in (
+        (z == 0, (last_above,)),
+        (z == CHIPS - 1, (last_below,)),
+        ((z > 0) & (z < CHIPS - 1), (last_below, last_above)),
+    ):
+        @pl.when(case)
+        def _(terms=terms):
+            total = last_own[...]
+            for term in terms:
+                total += term[...].astype(jnp.float32)
+            last[...] = total.astype(jnp.bfloat16)
+
+    copies[-1].start()
     for copy in copies:
         copy.wait()
 
@@ -430,12 +467,14 @@
         bf16 = jnp.bfloat16
         part = rows // CHUNKS
         hbm, vmem = pl.BlockSpec(memory_space=pl.ANY), pl.BlockSpec(memory_space=pltpu.VMEM)
-        held = [(rows, depth), (tokens, width), (tokens, width), (width, depth)]
+        fine = part // PIECES
+        held = [pltpu.VMEM(s, bf16) for s in ((rows, depth), (tokens, width), (tokens, width), (width, depth))]
+        held += [pltpu.VMEM((fine, depth), t) for t in (jnp.float32, bf16, bf16)]
         gathered = [(tokens, depth), (tokens, depth), (CHIPS, rows, depth), (CHIPS, rows, depth), (CHIPS, rows, depth)]
         dma = pltpu.SemaphoreType.DMA
         held_out = pl.pallas_call(
             kernel,
-            out_shape=[pltpu.VMEM(s, bf16) for s in held] + [jax.ShapeDtypeStruct(s, bf16) for s in gathered],
+            out_shape=held + [jax.ShapeDtypeStruct(s, bf16) for s in gathered],
             in_specs=[hbm] * 7,
             out_specs=[vmem] * len(held) + [hbm] * len(gathered),
             scratch_shapes=[
@@ -448,7 +487,7 @@
                 dma((2, 2 * CHIPS, CHUNKS)), dma((2, 3, CHIPS, CHUNKS)),
                 dma((CHIPS, CHUNKS)), dma((CHIPS, CHUNKS * PIECES)), dma((CHIPS, CHUNKS * PIECES)), dma((2 * CHUNKS,)),
             ],
-            compiler_params=pltpu.CompilerParams(collective_id=0, has_side_effects=True, vmem_limit_bytes=41 * 2**20),
+            compiler_params=pltpu.CompilerParams(collective_id=0, has_side_effects=True, vmem_limit_bytes=79 * 2**19),
             cost_estimate=pl.CostEstimate(flops=12 * tokens * depth * width, bytes_accessed=150 * 2**20, transcendentals=0),
         )(x, dy, gate, up, w_gate, w_up, w_down)[: len(held)]
         return pl.pallas_call(
@@ -456,8 +495,8 @@
             out_shape=[jax.ShapeDtypeStruct(s, bf16) for s in ((rows, depth), (depth, width), (depth, width), (width, depth))],
             in_specs=[vmem] * len(held),
             out_specs=[hbm] * 4,
-            scratch_shapes=[dma((4,))],
-            compiler_params=pltpu.CompilerParams(vmem_limit_bytes=2**20),
+            scratch_shapes=[pltpu.VMEM((fine, depth), bf16), dma((5,))],
+            compiler_params=pltpu.CompilerParams(vmem_limit_bytes=2 * 2**20),
         )(*held_out)
 
     whole, rows, cols = P(("dp", "tp"), None), P("tp", None), P(None, "tp")

time: 330 us -> 328 us (level)
  no operation moved by 1% of the time
where the time goes in v4:
time: 328 us; the launch traced here: 327 us
  Pallas kernels  326 us (99%)
    pallas_call x1, Pallas kernels, step(): pl.pallas_call(kernel, out_shape=held + [jax.ShapeDtypeStruct(s, bf16) fo...  321 us

profile of v4, /device:TPU:0, one launch (start us, length us, event | category | flops | bytes accessed | tf_op | source)
XLA Modules:
  0.0 326.8 jit_solution(7915624989772537559)
XLA Ops:
  0.6 320.9 %shard_map.102 = (bf16[512,2048]{1,0:T(8,128)(2,1)S(1)}, bf16[4096,1024]{1,0:T(8,128)(2,1)S(1)}, bf16[4096,1024]{1,0:T(8,128)(2,1)S(1)}, bf16[1024,2048]{1,0:T(8...) custom-call(bf16[512,2048]{1,0:T(8,128)(2,1)} %x.1, ...), custom_call_target="tpu_custom_call" | custom-call | flops 103079215104 | bytes 157286400 | tf_op jit(solution)/shard_map/pallas_call | solution.py:475
  321.6 5.2 %shard_map.103 = (bf16[512,2048]{1,0:T(8,128)(2,1)}, bf16[2048,1024]{1,0:T(8,128)(2,1)}, bf16[2048,1024]{1,0:T(8,128)(2,1)}, bf16[1024,2048]{1,0:T(8,128)(2,1)}) custom-call(bf16[512,2048]{1,0:T(8,128)(2,1)S(1)} %get-tuple-element.11.dx, bf16[4096,1024]{1,0:T(8,128)(2,1)S(1)} %get-tuple-element.12.dg, bf16[4096,1024]{1,0:T(8,128)(2,1)S(1)} %get-tuple-element.13.du, ...), custom_call_target="tpu_custom_call" | custom-call | tf_op jit(solution)/shard_map/pallas_call | solution.py:493
